TPU v7x, 32 devices: a whole 2x2x4 slice. The times are simulated.
32 devices in a mesh: blk: 16 (over z, y, x), rep: 2 (over core).
Axes of the slice: x: 2, y: 2, z: 4, core: 2. Of those that a mesh axis runs over, the one named last changes fastest.
Arguments:
- load_coef: bfloat16 [32, 2049, 256], P('blk', None, 'rep'), parts along dimension 2, may hold values from -0.29882812 to 0.29882812
- legendre: bfloat16 [32, 2049, 1024], P('blk'), may hold values from -0.125 to 0.125
- slab_orders: int32 [32], replicated, may hold values from 0 to 1023, as said below
- cycle_rows: int32 [1024], replicated, may hold values from 0 to 1023, each once
Outputs:
- potential: bfloat16 [1024, 128, 4096], P('blk', 'rep'), parts along dimension 1
- energy: float32 [128], P('rep'), parts along dimension 0
There are 2 independent parts, one for each index of `rep`. A program takes and returns all parts, laid end to end along the dimension named above; an argument that names none is the same for every part. Nothing has to cross between parts.
Inputs may be any that keep to these rules, and one draw needn't show every extreme that they name: `slab_orders`: values are distinct and below (2048) / 2. `cycle_rows`: each cycle appears once.
All inputs are finite; a program needn't handle non-finite values.
Results may differ from a plain program's by a relative error of at most 0.0055.
Values may be sent and summed in bfloat16 or wider, within the bound.
A program may use at most 192 MiB of HBM per device.

v0:
```python
import math
import jax
import jax.numpy as jnp
from jax import lax
from jax.sharding import PartitionSpec as P

NLON = 4096


def basis_rows(frequency):
    coarse_ids = jnp.arange(NLON // 64, dtype=jnp.int32) * 64
    fine_ids = jnp.arange(64, dtype=jnp.int32)
    scale = 2.0 * math.pi / NLON
    coarse_angles = (frequency[:, None] * coarse_ids[None, :] % NLON).astype(jnp.float32) * scale
    fine_angles = (frequency[:, None] * fine_ids[None, :] % NLON).astype(jnp.float32) * scale
    cos_coarse = jnp.cos(coarse_angles)[:, :, None]
    sin_coarse = jnp.sin(coarse_angles)[:, :, None]
    cos_fine = jnp.cos(fine_angles)[:, None, :]
    sin_fine = jnp.sin(fine_angles)[:, None, :]
    cosine = (cos_coarse * cos_fine - sin_coarse * sin_fine).reshape(frequency.shape[0], NLON)
    sine = (sin_coarse * cos_fine + cos_coarse * sin_fine).reshape(frequency.shape[0], NLON)
    factor = jnp.where(frequency == 0, 1.0, 2.0).astype(jnp.float32)[:, None]
    return ((factor * cosine).astype(jnp.bfloat16), (-factor * sine).astype(jnp.bfloat16))


def fourier(received, low_orders, degree):
    cos_lower, sin_lower = basis_rows(low_orders)
    cos_upper, sin_upper = basis_rows(degree - low_orders)
    fourier_basis = jnp.stack([cos_lower, sin_lower, cos_upper, sin_upper], axis=1)
    return jnp.einsum("rnsf,nsk->rfk", received, fourier_basis, preferred_element_type=jnp.float32)


def shards(load_coef, legendre, slab_orders, cycle_rows):
    blocks = lax.axis_size("blk")
    position = lax.axis_index("blk")
    pair_count = load_coef.shape[0]
    slab_rows = load_coef.shape[1]
    fields = load_coef.shape[2] // 2
    lat_count = legendre.shape[2]
    cycle_count = lat_count // blocks
    degree = slab_rows - 2
    my_orders = lax.dynamic_slice_in_dim(slab_orders, position * pair_count, pair_count)
    row_ids = jnp.arange(slab_rows, dtype=jnp.int32)
    spectra = []
    for pair_index in range(pair_count):
        in_lower = (row_ids < slab_rows - 1 - my_orders[pair_index])[:, None]
        pair_coef = load_coef[pair_index]
        nothing = jnp.zeros_like(pair_coef)
        stacked = jnp.concatenate(
            [jnp.where(in_lower, pair_coef, nothing), jnp.where(in_lower, nothing, pair_coef)],
            axis=1,
        )
        spectra.append(
            lax.dot_general(
                legendre[pair_index],
                stacked,
                (((0,), (0,)), ((), ())),
                preferred_element_type=jnp.float32,
            ).astype(jnp.bfloat16)
        )
    spectra = jnp.stack(spectra, axis=1).reshape(lat_count, pair_count, 4, fields)
    spectra = jnp.take(spectra, cycle_rows, axis=0)
    all_orders = slab_orders.reshape(blocks, pair_count)
    cycle_grid = jnp.zeros((cycle_count, fields, NLON), jnp.float32)
    for pair_index in range(pair_count):
        cycle_grid = cycle_grid + fourier(
            lax.all_to_all(
                spectra[:, pair_index : pair_index + 1],
                "blk",
                split_axis=0,
                concat_axis=1,
                tiled=True,
            ),
            low_orders=all_orders[:, pair_index],
            degree=degree,
        )
    partial_energy = jnp.sum(cycle_grid * cycle_grid, axis=(0, 2))
    summed = lax.psum(partial_energy, "blk")
    energy = summed / (lat_count * NLON)
    return (cycle_grid.astype(jnp.bfloat16), energy)


def solution(mesh):
    in_specs = (P("blk", None, "rep"), P("blk", None, None), P(), P())
    out_specs = (P("blk", "rep", None), P("rep"))
    return jax.shard_map(shards, mesh=mesh, in_specs=in_specs, out_specs=out_specs, check_vma=False)
```

profile of v0, /device:TPU:0, one launch (start us, length us, event | category | flops | bytes accessed | tf_op | source)
XLA Modules:
  0.0 187.0 jit_solution(15199914749275640568)
XLA Ops:
  0.6 0.7 compare_and_fusion
  2.0 0.7 dynamic_slice.3
  4.7 3.6 %fusion.90 = (bf16[1,2049,128]{2,0,1:T(2,128)(2,1)S(1)}, bf16[1,2049,128]{2,0,1:T(2,128)(2,1)S(1)}) fusion(bf16[2,2049,128]{2,0,1:T(2,128)(2,1)} %param.4), kind=kLoop, calls=%fused_computation.175 | loop fusion | bytes 2098176 | tf_op jit(solution)/shard_map/slice | solution.py:47
  8.3 17.4 %fusion.88 = (bf16[1,2049,1024]{2,0,1:T(2,128)(2,1)}, bf16[1,2049,1024]{2,0,1:T(2,128)(2,1)S(1)}) fusion(bf16[2,2049,1024]{2,0,1:T(2,128)(2,1)} %param.5), kind=kLoop, calls=%fused_computation.173 | loop fusion | bytes 16785408 | tf_op jit(solution)/shard_map/slice | solution.py:55
  25.7 1.9 %broadcast_select_fusion.2 = (bf16[2049,128]{1,0:T(8,128)(2,1)S(1)}, bf16[2049,128]{1,0:T(8,128)(2,1)S(1)}, bf16[2049,128]{1,0:T(8,128)(2,1)S(1)}, bf16[2049,128]{1,0:T(8,128)(2,1)S(1)}) fusion(pred[2049]{0:T(1024)(128)(4,1)S(1)} %iota_compare_fusion, bf16[1,2049,128]{2,0,1:T(2,128)(2,1)S(1)} %get-tuple-element.25, ...), kind=kLoop, calls=%fused_computation.25 | loop fusion | flops 1049088 | bytes 3151362 | tf_op jit(solution)/shard_map/jit(_where)/select_n | solution.py:50
  27.6 1.5 fusion.3
  29.2 0.7 copy.12
  29.9 4.9 %fusion.2 = bf16[256,1024]{1,0:T(8,128)(2,1)S(1)} fusion(bf16[1,2049,1024]{2,0,1:T(2,128)(2,1)} %get-tuple-element.16, bf16[2049,128]{1,0:T(8,128)(2,1)S(1)} %get-tuple-element.71, bf16[2049,128]{1,0:T(8,128)(2,1)S(1)} %get-tuple-element.72), kind=kOutput, calls=%fused_computation.9 | convolution fusion | flops 1076626432 | bytes 5769728 | tf_op jit(solution)/shard_map/dot_general | solution.py:54
  34.8 0.7 copy.11
  35.5 3.1 %pad_maximum_fusion = bf16[1024,2,4,64]{3,2,1,0:T(4,128)(2,1)} fusion(bf16[1024,1,4,64]{3,2,1,0:T(4,128)(2,1)S(1)} %copy.12, bf16[1024,1,4,64]{3,2,1,0:T(4,128)(2,1)S(1)} %copy.11), kind=kLoop, calls=%fused_computation.7 | loop fusion | flops 524288 | bytes 2097152 | tf_op jit(solution)/shard_map/stack | solution.py:61
  38.6 5.8 %gather_fusion = bf16[1024,2,4,64]{3,2,1,0:T(4,128)(2,1)S(1)} fusion(bf16[1024,2,4,64]{3,2,1,0:T(4,128)(2,1)} %pad_maximum_fusion, s32[1024]{0:T(1024)S(1)} %fusion.83), kind=kCustom, calls=%fused_computation | custom fusion | bytes 2101248 | tf_op jit(solution)/shard_map/jit(_take)/gather | solution.py:62
  44.4 3.8 %broadcast_select_fusion = bf16[1024,2,4,64]{3,2,1,0:T(4,128)(2,1)S(1)} fusion(bf16[1024,2,4,64]{3,2,1,0:T(4,128)(2,1)S(1)} %gather_fusion, pred[1024]{0:T(1024)(128)(4,1)S(1)} %compare_and_fusion), kind=kLoop, calls=%fused_computation.8 | loop fusion | flops 524288 | bytes 2098176 | tf_op jit(solution)/shard_map/jit(_take)/select_n | solution.py:62
  48.3 0.7 fusion.89
  49.0 1.5 reshape.1147
  50.5 8.3 %all-to-all-start = ((bf16[16,2,8192]{2,1,0:T(2,128)(2,1)}), bf16[16,2,8192]{2,1,0:T(2,128)(2,1)S(1)}, u32[]{:S(2)}, u32[]{:S(2)}) async-start(bf16[16,2,8192]{2,1,0:T(2,128)(2,1)} %reshape.1147), calls=%async_computation | async-start | bytes 1048576 | tf_op jit(solution)/shard_map/all_to_all | solution.py:67
  59.6 1.4 multiply_subtract_fusion
  61.0 1.9 %sub.99 = f32[16,1,4096]{2,0,1:T(8,128)} reshape(f32[16,64,64]{2,1,0:T(8,128)} %get-tuple-element.28) | data formatting | bytes 524288 | tf_op jit(solution)/shard_map/sub | solution.py:20
  62.9 0.9 add.180
  63.8 0.9 add.176
  64.9 1.4 multiply_subtract_fusion.2
  66.3 1.9 %sub.93 = f32[16,1,4096]{2,0,1:T(8,128)} reshape(f32[16,64,64]{2,1,0:T(8,128)} %get-tuple-element.32) | data formatting | bytes 524288 | tf_op jit(solution)/shard_map/sub | solution.py:20
  68.2 0.9 add.172
  69.6 1.0 multiply_convert_fusion.1
  70.7 1.7 multiply_convert_fusion
  72.3 1.7 multiply_convert_fusion.2
  74.0 0.7 multiply_convert_fusion.3
  74.7 1.0 multiply_convert_fusion.5
  76.1 1.5 reshape.1149
  77.8 6.9 %all-to-all-start.1 = ((bf16[16,2,8192]{2,1,0:T(2,128)(2,1)}), bf16[16,2,8192]{2,1,0:T(2,128)(2,1)S(1)}, u32[]{:S(2)}, u32[]{:S(2)}) async-start(bf16[16,2,8192]{2,1,0:T(2,128)(2,1)} %reshape.1149), calls=%async_computation.1 | async-start | bytes 1048576 | tf_op jit(solution)/shard_map/all_to_all | solution.py:67
  85.4 23.2 %fusion.11 = f32[64,64,4096,1]{2,1,3,0:T(8,128)} fusion(bf16[16,64,1,4,64]{4,3,1,0,2:T(4,128)(2,1)S(1)} %bitcast.61, bf16[16,1,4096]{2,0,1:T(8,128)(2,1)S(1)} %multiply_convert_fusion.4, bf16[16,1,4096]{2,0,1:T(8,128)(2,1)S(1)} %multiply_convert_fusion.5, bf16[16,1,4096]{2,0,1:T(8,128)(2,1)S(1)} %multiply_convert_fusion.6, ...), kind=kOutput, calls=%fused_computation.18 | convolution fusion | flops 2148270080 | bytes 68157440 | tf_op jit(solution)/shard_map/rnsf,nsk->rfk/dot_general | solution.py:30
  109.3 35.2 %multiply_reduce_fusion = (f32[64]{0:T(128)S(1)}, bf16[64,64,4096]{2,1,0:T(8,128)(2,1)}) fusion(bf16[16,1,4096]{2,0,1:T(8,128)(2,1)S(1)} %copy-done.1, bf16[16,1,4096]{2,0,1:T(8,128)(2,1)S(1)} %multiply_convert_fusion.1, bf16[16,1,4096]{2,0,1:T(8,128)(2,1)S(1)} %copy-done.2, bf16[16,1,4096]{2,0,1:T(8,128)(2,1)S(1)} %copy-done.3, ...), kind=kOutput, calls=%fused_computation.2 | convolution fusion | flops 2215378944 | bytes 101712128 | tf_op jit(solution)/shard_map/rnsf,nsk->rfk/dot_general | solution.py:30
  144.4 42.1 %psum.7 = f32[64]{0:T(128)S(1)} all-reduce(f32[64]{0:T(128)S(1)} %get-tuple-element.14), channel_id=1, replica_groups=mesh['blk'=16,'rep'=2] {'blk'}, use_global_device_ids=true, to_apply=%region_1.2 | all-reduce | flops 64 | bytes 512 | tf_op jit(solution)/shard_map/psum | solution.py:78
  (32 shorter events, 5.0 us)
Async XLA Ops:
  49.0 9.9 %copy-start.4 = (s32[32]{0:T(128)S(1)}, s32[32]{0:T(128)}, u32[]{:S(2)}) copy-start(s32[32]{0:T(128)} %param.6) | copy-start | bytes 388
  50.5 27.2 %all-to-all-start = ((bf16[16,2,8192]{2,1,0:T(2,128)(2,1)}), bf16[16,2,8192]{2,1,0:T(2,128)(2,1)S(1)}, u32[]{:S(2)}, u32[]{:S(2)}) async-start(bf16[16,2,8192]{2,1,0:T(2,128)(2,1)} %reshape.1147), calls=%async_computation | async-start | bytes 1048576 | tf_op jit(solution)/shard_map/all_to_all | solution.py:67
  69.1 6.7 %copy-start = (f32[16,1,4096]{2,0,1:T(8,128)S(1)}, f32[16,1,4096]{2,0,1:T(8,128)}, u32[]{:S(2)}) copy-start(f32[16,1,4096]{2,0,1:T(8,128)} %add.172) | copy-start | bytes 786436
  77.8 30.8 %all-to-all-start.1 = ((bf16[16,2,8192]{2,1,0:T(2,128)(2,1)}), bf16[16,2,8192]{2,1,0:T(2,128)(2,1)S(1)}, u32[]{:S(2)}, u32[]{:S(2)}) async-start(bf16[16,2,8192]{2,1,0:T(2,128)(2,1)} %reshape.1149), calls=%async_computation.1 | async-start | bytes 1048576 | tf_op jit(solution)/shard_map/all_to_all | solution.py:67
  85.3 23.9 %copy-start.1 = (bf16[16,1,4096]{2,0,1:T(8,128)(2,1)S(1)}, bf16[16,1,4096]{2,0,1:T(8,128)(2,1)}, u32[]{:S(2)}) copy-start(bf16[16,1,4096]{2,0,1:T(8,128)(2,1)} %multiply_convert_fusion) | copy-start | bytes 393220
  85.3 23.9 %copy-start.2 = (bf16[16,1,4096]{2,0,1:T(8,128)(2,1)S(1)}, bf16[16,1,4096]{2,0,1:T(8,128)(2,1)}, u32[]{:S(2)}) copy-start(bf16[16,1,4096]{2,0,1:T(8,128)(2,1)} %multiply_convert_fusion.2) | copy-start | bytes 393220
  85.4 23.9 %copy-start.3 = (bf16[16,1,4096]{2,0,1:T(8,128)(2,1)S(1)}, bf16[16,1,4096]{2,0,1:T(8,128)(2,1)}, u32[]{:S(2)}) copy-start(bf16[16,1,4096]{2,0,1:T(8,128)(2,1)} %multiply_convert_fusion.3) | copy-start | bytes 393220
where the time goes:
time: 188 us; the launch traced here: 187 us
  matrix products  64.8 us (34%)
  blocking collectives  42.1 us (22%)
  local copies, waits for them, and re-layouts  41.8 us (22%)
  other arithmetic  20.9 us (11%)
  starting transfers between devices  15.3 us (8%)
  between operations  2.17 us (1%)
    dot_general x2, matrix products, fourier(): jnp.einsum('rnsf,nsk->rfk', received, fourier_basis, preferred_element_ty...  58.4 us
    psum x1, blocking collectives, shards(): summed = lax.psum(partial_energy, 'blk')  42.1 us
    slice x1, local copies, waits for them, and re-layouts, shards(): legendre[pair_index]  17.4 us
    all_to_all x2, starting transfers between devices, shards(): lax.all_to_all(spectra[:, pair_index:pair_index + 1], 'blk', split_axis=0...  15.3 us
    dot_general x2, matrix products, shards(): lax.dot_general(legendre[pair_index], stacked, (((0,), (0,)), ((), ())),...  6.43 us
    gather x1, local copies, waits for them, and re-layouts, shards(): spectra = jnp.take(spectra, cycle_rows, axis=0)  5.81 us
    unnamed x14, local copies, waits for them, and re-layouts  4.35 us
    sub x4, local copies, waits for them, and re-layouts, basis_rows(): cos_coarse * cos_fine - sin_coarse * sin_fine  4.24 us
  transfers between devices with their start and end apart: 2, of which 0 were waited for; matrix products, arithmetic and copies ran while one was open for 23% of the time, Pallas kernels for 0%

commit v1 on v0

--- a/solution.py
+++ b/solution.py
@@ -5,6 +5,12 @@
 from jax.sharding import PartitionSpec as P
 
 NLON = 4096
+
+
+def trade_parts(x, axis, split, join):
+    shards = jnp.split(x, lax.axis_size(axis), axis=split)
+    received = lax.all_to_all(jnp.stack(shards), axis, 0, 0)
+    return jnp.concatenate(received, axis=join)
 
 
 def basis_rows(frequency):
@@ -64,13 +70,7 @@
     cycle_grid = jnp.zeros((cycle_count, fields, NLON), jnp.float32)
     for pair_index in range(pair_count):
         cycle_grid = cycle_grid + fourier(
-            lax.all_to_all(
-                spectra[:, pair_index : pair_index + 1],
-                "blk",
-                split_axis=0,
-                concat_axis=1,
-                tiled=True,
-            ),
+            trade_parts(spectra[:, pair_index : pair_index + 1], "blk", 0, 1),
             low_orders=all_orders[:, pair_index],
             degree=degree,
         )

time: 188 us -> 204 us (1.085)
  waiting for transfers between devices: 0.01 us -> 12.7 us
  blocking collectives: 42.1 us -> 39.1 us
  local copies, waits for them, and re-layouts: 41.8 us -> 44.6 us
  other arithmetic: 20.9 us -> 23.4 us
    all_to_all x2, waiting for transfers between devices: 0.01 us -> 12.7 us  [trade_parts(): received = lax.all_to_all(jnp.stack(shards), axis, 0, 0)]
    psum x1, blocking collectives: 42.1 us -> 39.1 us  [shards(): summed = lax.psum(partial_energy, 'blk')]
    gather x1, local copies, waits for them, and re-layouts: 5.81 us -> 8.55 us  [shards(): spectra = jnp.take(spectra, cycle_rows, axis=0)]
    sub x4, local copies, waits for them, and re-layouts: 4.24 us -> 2.13 us  [basis_rows(): cos_coarse * cos_fine - sin_coarse * sin_fine]
    unnamed x14 -> x74, local copies, waits for them, and re-layouts: 4.35 us -> 6.22 us
  transfers between devices with their start and end apart: 2 -> 2, of which waited for: 0 -> 1; matrix products, arithmetic and copies ran while one was open for 23% -> 10% of each run, Pallas kernels for 0% -> 0%
where the time goes in v1:
time: 204 us; the launch traced here: 203 us
  matrix products  65.6 us (32%)
  local copies, waits for them, and re-layouts  44.6 us (22%)
  blocking collectives  39.1 us (19%)
  other arithmetic  23.4 us (11%)
  starting transfers between devices  15.3 us (8%)
  waiting for transfers between devices  12.7 us (6%)
  between operations  2.47 us (1%)
    dot_general x2, matrix products, fourier(): jnp.einsum('rnsf,nsk->rfk', received, fourier_basis, preferred_element_ty...  59.1 us
    psum x1, blocking collectives, shards(): summed = lax.psum(partial_energy, 'blk')  39.1 us
    slice x1, local copies, waits for them, and re-layouts, shards(): legendre[pair_index]  17.4 us
    all_to_all x2, starting transfers between devices, trade_parts(): received = lax.all_to_all(jnp.stack(shards), axis, 0, 0)  15.3 us
    all_to_all x2, waiting for transfers between devices, trade_parts(): received = lax.all_to_all(jnp.stack(shards), axis, 0, 0)  12.7 us
    gather x1, local copies, waits for them, and re-layouts, shards(): spectra = jnp.take(spectra, cycle_rows, axis=0)  8.55 us
    dot_general x2, matrix products, shards(): lax.dot_general(legendre[pair_index], stacked, (((0,), (0,)), ((), ())),...  6.43 us
    unnamed x74, local copies, waits for them, and re-layouts  6.22 us
  transfers between devices with their start and end apart: 2, of which 1 were waited for; matrix products, arithmetic and copies ran while one was open for 10% of the time, Pallas kernels for 0%

profile of v1, /device:TPU:0, one launch (start us, length us, event | category | flops | bytes accessed | tf_op | source)
XLA Modules:
  0.0 203.2 jit_solution(15300780508807899598)
XLA Ops:
  2.0 0.7 dynamic_slice.3
  4.7 3.6 %fusion.106 = (bf16[1,2049,128]{2,0,1:T(2,128)(2,1)S(1)}, bf16[1,2049,128]{2,0,1:T(2,128)(2,1)S(1)}) fusion(bf16[2,2049,128]{2,0,1:T(2,128)(2,1)} %param.4), kind=kLoop, calls=%fused_computation.222 | loop fusion | bytes 2098176 | tf_op jit(solution)/shard_map/slice | solution.py:53
  8.3 17.4 %fusion.104 = (bf16[1,2049,1024]{2,0,1:T(2,128)(2,1)}, bf16[1,2049,1024]{2,0,1:T(2,128)(2,1)S(1)}) fusion(bf16[2,2049,1024]{2,0,1:T(2,128)(2,1)} %param.5), kind=kLoop, calls=%fused_computation.220 | loop fusion | bytes 16785408 | tf_op jit(solution)/shard_map/slice | solution.py:61
  25.7 1.9 bitcast_select_fusion.1
  27.6 1.5 fusion.3
  29.9 4.9 %fusion.2 = bf16[256,1024]{1,0:T(8,128)(2,1)S(1)} fusion(bf16[1,2049,1024]{2,0,1:T(2,128)(2,1)} %get-tuple-element.16, bf16[2049,128]{1,0:T(8,128)(2,1)S(1)} %get-tuple-element.35, bf16[2049,128]{1,0:T(8,128)(2,1)S(1)} %get-tuple-element.34), kind=kOutput, calls=%fused_computation.9 | convolution fusion | flops 1076626432 | bytes 5769728 | tf_op jit(solution)/shard_map/dot_general | solution.py:60
  34.8 1.4 copy.1406
  36.2 3.0 %pad_maximum_fusion = bf16[1024,2,4,64]{3,2,1,0:T(4,128)(2,1)S(1)} fusion(bf16[1024,1,4,64]{3,2,1,0:T(4,128)(2,1)S(1)} %copy.1407, bf16[1024,1,4,64]{3,2,1,0:T(4,128)(2,1)} %copy.1406), kind=kLoop, calls=%fused_computation.7 | loop fusion | flops 524288 | bytes 2097152 | tf_op jit(solution)/shard_map/stack | solution.py:67
  39.2 8.6 %gather_fusion = bf16[1024,2,4,64]{3,2,1,0:T(4,128)(2,1)} fusion(bf16[1024,2,4,64]{3,2,1,0:T(4,128)(2,1)S(1)} %pad_maximum_fusion, s32[1024]{0:T(1024)S(1)} %fusion.99), kind=kCustom, calls=%fused_computation | custom fusion | bytes 2101248 | tf_op jit(solution)/shard_map/jit(_take)/gather | solution.py:68
  47.8 5.2 %broadcast_select_fusion = bf16[1024,2,4,64]{3,2,1,0:T(4,128)(2,1)S(1)} fusion(bf16[1024,2,4,64]{3,2,1,0:T(4,128)(2,1)} %gather_fusion, pred[1024]{0:T(1024)(128)(4,1)S(1)} %compare_and_fusion), kind=kLoop, calls=%fused_computation.8 | loop fusion | flops 524288 | bytes 2098176 | tf_op jit(solution)/shard_map/jit(_take)/select_n | solution.py:68
  53.7 1.5 reshape.1165
  55.2 8.3 %all-to-all-start.1 = ((bf16[16,2,8192]{2,1,0:T(2,128)(2,1)}), bf16[16,2,8192]{2,1,0:T(2,128)(2,1)S(1)}, u32[]{:S(2)}, u32[]{:S(2)}) async-start(bf16[16,2,8192]{2,1,0:T(2,128)(2,1)} %reshape.1165), calls=%async_computation.1 | async-start | bytes 1048576 | tf_op jit(solution)/shard_map/all_to_all | solution.py:12
  64.5 1.2 fusion.105
  65.8 1.0 fusion.92
  67.3 0.9 sub.99
  68.8 1.4 multiply_subtract_fusion.2
  70.2 0.9 sub.93
  71.1 0.9 add.172
  72.1 1.0 constant_dynamic-update-slice_fusion.15
  73.0 0.8 select_reduce_fusion
  73.9 0.8 select_reduce_fusion.2
  74.7 1.7 multiply_convert_fusion.1
  77.1 0.7 multiply_convert_fusion.2
  77.8 0.7 multiply_convert_fusion.3
  78.6 1.0 multiply_convert_fusion.5
  80.6 1.5 reshape.1163
  82.2 6.9 %all-to-all-start = ((bf16[16,2,8192]{2,1,0:T(2,128)(2,1)}), bf16[16,2,8192]{2,1,0:T(2,128)(2,1)S(1)}, u32[]{:S(2)}, u32[]{:S(2)}) async-start(bf16[16,2,8192]{2,1,0:T(2,128)(2,1)} %reshape.1163), calls=%async_computation | async-start | bytes 1048576 | tf_op jit(solution)/shard_map/all_to_all | solution.py:12
  89.1 0.7 multiply_convert_fusion.7
  90.9 12.7 %all-to-all-done = bf16[16,2,8192]{2,1,0:T(2,128)(2,1)S(1)} async-done(((bf16[16,2,8192]{2,1,0:T(2,128)(2,1)}), bf16[16,2,8192]{2,1,0:T(2,128)(2,1)S(1)}, u32[]{:S(2)}, u32[]{:S(2)}) %all-to-all-start) | async-done | bytes 524320 | tf_op jit(solution)/shard_map/all_to_all | solution.py:12
  104.4 24.0 %fusion.11 = f32[64,64,4096,1]{2,1,3,0:T(8,128)} fusion(bf16[64,16,1,4,64]{4,0,3,2,1:T(8,128)(2,1)S(1)} %bitcast_bitcast_fusion.1, bf16[16,1,4096]{2,0,1:T(8,128)(2,1)S(1)} %multiply_convert_fusion.4, bf16[16,1,4096]{2,0,1:T(8,128)(2,1)S(1)} %multiply_convert_fusion.5, bf16[16,1,4096]{2,0,1:T(8,128)(2,1)S(1)} %multiply_convert_fusion.6, ...), kind=kOutput, calls=%fused_computation.18 | convolution fusion | flops 2148270080 | bytes 68157440 | tf_op jit(solution)/shard_map/rnsf,nsk->rfk/dot_general | solution.py:36
  128.4 35.2 %multiply_reduce_fusion = (f32[64]{0:T(128)S(1)}, bf16[64,64,4096]{2,1,0:T(8,128)(2,1)}) fusion(bf16[16,1,4096]{2,0,1:T(8,128)(2,1)S(1)} %copy-done.3, bf16[16,1,4096]{2,0,1:T(8,128)(2,1)S(1)} %copy-done.2, bf16[16,1,4096]{2,0,1:T(8,128)(2,1)S(1)} %copy-done.4, bf16[16,1,4096]{2,0,1:T(8,128)(2,1)S(1)} %copy-done.5, ...), kind=kOutput, calls=%fused_computation.2 | convolution fusion | flops 2215378944 | bytes 101712128 | tf_op jit(solution)/shard_map/rnsf,nsk->rfk/dot_general | solution.py:36
  163.6 39.1 %psum.7 = f32[64]{0:T(128)S(1)} all-reduce(f32[64]{0:T(128)S(1)} %get-tuple-element.14), channel_id=1, replica_groups=mesh['blk'=16,'rep'=2] {'blk'}, use_global_device_ids=true, to_apply=%region_1.2 | all-reduce | flops 64 | bytes 512 | tf_op jit(solution)/shard_map/psum | solution.py:78
  (96 shorter events, 9.4 us)
Async XLA Ops:
  53.2 10.4 %copy-start.19 = (s32[32]{0:T(128)S(1)}, s32[32]{0:T(128)}, u32[]{:S(2)}) copy-start(s32[32]{0:T(128)} %param.6) | copy-start | bytes 388
  55.2 27.0 %all-to-all-start.1 = ((bf16[16,2,8192]{2,1,0:T(2,128)(2,1)}), bf16[16,2,8192]{2,1,0:T(2,128)(2,1)S(1)}, u32[]{:S(2)}, u32[]{:S(2)}) async-start(bf16[16,2,8192]{2,1,0:T(2,128)(2,1)} %reshape.1165), calls=%async_computation.1 | async-start | bytes 1048576 | tf_op jit(solution)/shard_map/all_to_all | solution.py:12
  72.0 7.6 %copy-start = (f32[16,1,4096]{2,0,1:T(8,128)S(1)}, f32[16,1,4096]{2,0,1:T(8,128)}, u32[]{:S(2)}) copy-start(f32[16,1,4096]{2,0,1:T(8,128)} %add.172) | copy-start | bytes 786436
  72.0 7.7 %copy-start.18 = (bf16[64,1,4,64]{3,2,1,0:T(4,128)(2,1)S(1)}, bf16[64,1,4,64]{3,2,1,0:T(4,128)(2,1)}, u32[]{:S(2)}) copy-start(bf16[64,1,4,64]{3,2,1,0:T(4,128)(2,1)} %get-tuple-element.32) | copy-start | bytes 98308
  72.0 7.8 %copy-start.17 = (bf16[64,1,4,64]{3,2,1,0:T(4,128)(2,1)S(1)}, bf16[64,1,4,64]{3,2,1,0:T(4,128)(2,1)}, u32[]{:S(2)}) copy-start(bf16[64,1,4,64]{3,2,1,0:T(4,128)(2,1)} %get-tuple-element.31) | copy-start | bytes 98308
  72.0 7.8 %copy-start.16 = (bf16[64,1,4,64]{3,2,1,0:T(4,128)(2,1)S(1)}, bf16[64,1,4,64]{3,2,1,0:T(4,128)(2,1)}, u32[]{:S(2)}) copy-start(bf16[64,1,4,64]{3,2,1,0:T(4,128)(2,1)} %get-tuple-element.30) | copy-start | bytes 98308
  72.0 7.8 %copy-start.15 = (bf16[64,1,4,64]{3,2,1,0:T(4,128)(2,1)S(1)}, bf16[64,1,4,64]{3,2,1,0:T(4,128)(2,1)}, u32[]{:S(2)}) copy-start(bf16[64,1,4,64]{3,2,1,0:T(4,128)(2,1)} %get-tuple-element.29) | copy-start | bytes 98308
  72.0 7.9 %copy-start.14 = (bf16[64,1,4,64]{3,2,1,0:T(4,128)(2,1)S(1)}, bf16[64,1,4,64]{3,2,1,0:T(4,128)(2,1)}, u32[]{:S(2)}) copy-start(bf16[64,1,4,64]{3,2,1,0:T(4,128)(2,1)} %get-tuple-element.28) | copy-start | bytes 98308
  72.0 7.9 %copy-start.13 = (bf16[64,1,4,64]{3,2,1,0:T(4,128)(2,1)S(1)}, bf16[64,1,4,64]{3,2,1,0:T(4,128)(2,1)}, u32[]{:S(2)}) copy-start(bf16[64,1,4,64]{3,2,1,0:T(4,128)(2,1)} %get-tuple-element.27) | copy-start | bytes 98308
  72.0 7.9 %copy-start.12 = (bf16[64,1,4,64]{3,2,1,0:T(4,128)(2,1)S(1)}, bf16[64,1,4,64]{3,2,1,0:T(4,128)(2,1)}, u32[]{:S(2)}) copy-start(bf16[64,1,4,64]{3,2,1,0:T(4,128)(2,1)} %get-tuple-element.26) | copy-start | bytes 98308
  72.0 7.9 %copy-start.11 = (bf16[64,1,4,64]{3,2,1,0:T(4,128)(2,1)S(1)}, bf16[64,1,4,64]{3,2,1,0:T(4,128)(2,1)}, u32[]{:S(2)}) copy-start(bf16[64,1,4,64]{3,2,1,0:T(4,128)(2,1)} %get-tuple-element.25) | copy-start | bytes 98308
  72.0 8.0 %copy-start.10 = (bf16[64,1,4,64]{3,2,1,0:T(4,128)(2,1)S(1)}, bf16[64,1,4,64]{3,2,1,0:T(4,128)(2,1)}, u32[]{:S(2)}) copy-start(bf16[64,1,4,64]{3,2,1,0:T(4,128)(2,1)} %get-tuple-element.24) | copy-start | bytes 98308
  72.0 8.0 %copy-start.9 = (bf16[64,1,4,64]{3,2,1,0:T(4,128)(2,1)S(1)}, bf16[64,1,4,64]{3,2,1,0:T(4,128)(2,1)}, u32[]{:S(2)}) copy-start(bf16[64,1,4,64]{3,2,1,0:T(4,128)(2,1)} %get-tuple-element.23) | copy-start | bytes 98308
  72.0 8.0 %copy-start.8 = (bf16[64,1,4,64]{3,2,1,0:T(4,128)(2,1)S(1)}, bf16[64,1,4,64]{3,2,1,0:T(4,128)(2,1)}, u32[]{:S(2)}) copy-start(bf16[64,1,4,64]{3,2,1,0:T(4,128)(2,1)} %get-tuple-element.22) | copy-start | bytes 98308
  72.1 8.0 %copy-start.7 = (bf16[64,1,4,64]{3,2,1,0:T(4,128)(2,1)S(1)}, bf16[64,1,4,64]{3,2,1,0:T(4,128)(2,1)}, u32[]{:S(2)}) copy-start(bf16[64,1,4,64]{3,2,1,0:T(4,128)(2,1)} %get-tuple-element.21) | copy-start | bytes 98308
  72.1 8.1 %copy-start.6 = (bf16[64,1,4,64]{3,2,1,0:T(4,128)(2,1)S(1)}, bf16[64,1,4,64]{3,2,1,0:T(4,128)(2,1)}, u32[]{:S(2)}) copy-start(bf16[64,1,4,64]{3,2,1,0:T(4,128)(2,1)} %get-tuple-element.20) | copy-start | bytes 98308
  82.2 21.4 %all-to-all-start = ((bf16[16,2,8192]{2,1,0:T(2,128)(2,1)}), bf16[16,2,8192]{2,1,0:T(2,128)(2,1)S(1)}, u32[]{:S(2)}, u32[]{:S(2)}) async-start(bf16[16,2,8192]{2,1,0:T(2,128)(2,1)} %reshape.1163), calls=%async_computation | async-start | bytes 1048576 | tf_op jit(solution)/shard_map/all_to_all | solution.py:12
  90.9 13.5 %copy-start.1 = (bf16[16,1,4096]{2,0,1:T(8,128)(2,1)S(1)}, bf16[16,1,4096]{2,0,1:T(8,128)(2,1)}, u32[]{:S(2)}) copy-start(bf16[16,1,4096]{2,0,1:T(8,128)(2,1)} %multiply_convert_fusion.7) | copy-start | bytes 393220
  104.4 24.0 %copy-start.2 = (bf16[16,1,4096]{2,0,1:T(8,128)(2,1)S(1)}, bf16[16,1,4096]{2,0,1:T(8,128)(2,1)}, u32[]{:S(2)}) copy-start(bf16[16,1,4096]{2,0,1:T(8,128)(2,1)} %multiply_convert_fusion.1) | copy-start | bytes 393220
  104.4 24.0 %copy-start.3 = (bf16[16,1,4096]{2,0,1:T(8,128)(2,1)S(1)}, bf16[16,1,4096]{2,0,1:T(8,128)(2,1)}, u32[]{:S(2)}) copy-start(bf16[16,1,4096]{2,0,1:T(8,128)(2,1)} %multiply_convert_fusion) | copy-start | bytes 393220
  104.4 24.0 %copy-start.4 = (bf16[16,1,4096]{2,0,1:T(8,128)(2,1)S(1)}, bf16[16,1,4096]{2,0,1:T(8,128)(2,1)}, u32[]{:S(2)}) copy-start(bf16[16,1,4096]{2,0,1:T(8,128)(2,1)} %multiply_convert_fusion.2) | copy-start | bytes 393220
  104.4 24.0 %copy-start.5 = (bf16[16,1,4096]{2,0,1:T(8,128)(2,1)S(1)}, bf16[16,1,4096]{2,0,1:T(8,128)(2,1)}, u32[]{:S(2)}) copy-start(bf16[16,1,4096]{2,0,1:T(8,128)(2,1)} %multiply_convert_fusion.3) | copy-start | bytes 393220
